TPU v7x, 32 devices: a 4x4x1 block of a 4x4x8 slice. The times are simulated.
32 devices in a mesh: data: 1 (over z), expert: 32 (over y, x, core).
Axes of the slice: x: 4, y: 4, z: 1, core: 2. Of those that a mesh axis runs over, the one named last changes fastest.
The devices are a block of a 4x4x8 slice.
Arguments:
- disp_one: bfloat16 [32, 64, 16, 2048], P('data', 'expert')
- slot_one: int32 [2048, 6], P(('data', 'expert'))
- expert_one: int32 [2048, 6], P(('data', 'expert'))
- gate_one: float32 [2048, 6], P(('data', 'expert'))
- disp_two: bfloat16 [32, 64, 16, 2048], P('data', 'expert')
- slot_two: int32 [2048, 6], P(('data', 'expert'))
- expert_two: int32 [2048, 6], P(('data', 'expert'))
- gate_two: float32 [2048, 6], P(('data', 'expert'))
- w_gate: bfloat16 [64, 2048, 1408], P('expert')
- w_up: bfloat16 [64, 2048, 1408], P('expert')
- w_down: bfloat16 [64, 1408, 2048], P('expert')
Outputs:
- output 1: bfloat16 [2048, 2048], P(('data', 'expert'))
- output 2: bfloat16 [2048, 2048], P(('data', 'expert'))
All inputs are finite; a program needn't handle non-finite values.
Results may differ from a plain program's by a relative error of at most 0.0015.
Values are sent between devices in bfloat16 or wider.
A program may use at most 768 MiB of HBM per device.

v0:
```python
import jax
import jax.numpy as jnp
from jax import lax
from jax.sharding import PartitionSpec as P


def expert_ffn(dispatched, w_gate, w_up, w_down):
    gate_act = jnp.einsum('secd,edf->secf', dispatched, w_gate, preferred_element_type=jnp.float32)
    up_act = jnp.einsum('secd,edf->secf', dispatched, w_up, preferred_element_type=jnp.float32)
    hidden = (jax.nn.silu(gate_act) * up_act).astype(jnp.bfloat16)
    return jnp.einsum('secf,efd->secd', hidden, w_down, preferred_element_type=jnp.float32).astype(jnp.bfloat16)


def combine_rows(returned, slot_ids, expert_ids, gates):
    capacity = returned.shape[-2]
    row_table = returned.reshape(-1, returned.shape[-1])
    row_index = expert_ids * capacity + jnp.maximum(slot_ids, 0)
    picked = jnp.take(row_table, row_index, axis=0)
    kept = jnp.where(slot_ids >= 0, gates, 0.0)
    return jnp.sum(kept[:, :, None] * picked, axis=1).astype(jnp.bfloat16)


def solution(mesh):
    disp_spec = P('data', 'expert', None, None)
    tok_spec = P(('data', 'expert'), None)
    weight_spec = P('expert', None, None)

    def local_step(disp_one, slot_one, expert_one, gate_one, disp_two, slot_two, expert_two, gate_two, w_gate, w_up, w_down):
        outputs = []
        batches = ((disp_one, slot_one, expert_one, gate_one), (disp_two, slot_two, expert_two, gate_two))
        for dispatched, slot_ids, expert_ids, gates in batches:
            y_rows = expert_ffn(dispatched, w_gate, w_up, w_down)
            returned = lax.all_to_all(y_rows, 'expert', 0, 0, tiled=True)
            outputs.append(combine_rows(returned, slot_ids, expert_ids, gates))
        return tuple(outputs)

    in_specs = (disp_spec, tok_spec, tok_spec, tok_spec, disp_spec, tok_spec, tok_spec, tok_spec,
                weight_spec, weight_spec, weight_spec)
    return jax.shard_map(local_step, mesh=mesh, in_specs=in_specs, out_specs=(tok_spec, tok_spec), check_vma=False)
```

profile of v0, /device:TPU:103, one launch (start us, length us, event | category | flops | bytes accessed | tf_op | source)
XLA Modules:
  0.0 183.9 jit_solution(18373660831070355378)
XLA Ops:
  0.6 14.4 %bitcast_multiply_fusion.3 = f32[32,2,16,1408]{3,0,2,1:T(8,128)} fusion(bf16[2,2048,1408]{2,1,0:T(8,128)(2,1)} %param.21, bf16[32,2,16,2048]{3,2,1,0:T(8,128)(2,1)} %param.13), kind=kOutput, calls=%fused_computation.23 | convolution fusion | flops 5911347200 | bytes 21495808 | tf_op jit(solution)/shard_map/secd,edf->secf/dot_general | solution.py:8
  15.0 15.8 %fusion.18 = bf16[32,2,16,1408]{3,0,2,1:T(8,128)(2,1)S(1)} fusion(f32[32,2,16,1408]{3,0,2,1:T(8,128)} %bitcast_multiply_fusion.3, bf16[2,2048,1408]{2,1,0:T(8,128)(2,1)} %param.22, bf16[32,2,16,2048]{3,2,1,0:T(8,128)(2,1)} %param.13), kind=kOutput, calls=%fused_computation.22 | convolution fusion | flops 5908463616 | bytes 24379392 | tf_op jit(solution)/shard_map/secd,edf->secf/dot_general | solution.py:9
  30.8 9.5 %convert_bitcast_fusion.1 = bf16[32,2,16,2048]{3,2,0,1:T(8,128)(2,1)S(1)} fusion(bf16[2,1408,2048]{2,1,0:T(8,128)(2,1)} %param.23, bf16[32,2,16,1408]{3,0,2,1:T(8,128)(2,1)S(1)} %fusion.18), kind=kOutput, calls=%fused_computation.31 | convolution fusion | flops 5907677184 | bytes 18612224 | tf_op jit(solution)/shard_map/secf,efd->secd/dot_general | solution.py:11
  40.3 2.7 %copy.38 = bf16[32,2,16,2048]{3,2,1,0:T(8,128)(2,1)} copy(bf16[32,2,16,2048]{3,2,0,1:T(8,128)(2,1)S(1)} %convert_bitcast_fusion.1) | data formatting | bytes 8388608 | tf_op jit(solution)/shard_map/convert_element_type | solution.py:11
  43.0 8.0 %all-to-all-start = ((bf16[32,2,16,2048]{3,2,1,0:T(8,128)(2,1)}), bf16[32,2,16,2048]{3,2,1,0:T(8,128)(2,1)}, u32[]{:S(2)}, u32[]{:S(2)}) async-start(bf16[32,2,16,2048]{3,2,1,0:T(8,128)(2,1)} %copy.38), calls=%async_computation | async-start | bytes 8388608 | tf_op jit(solution)/shard_map/all_to_all | solution.py:33
  51.0 14.4 %bitcast_multiply_fusion.1 = f32[32,2,16,1408]{3,0,2,1:T(8,128)} fusion(bf16[2,2048,1408]{2,1,0:T(8,128)(2,1)} %param.21, bf16[32,2,16,2048]{3,2,1,0:T(8,128)(2,1)} %param.17), kind=kOutput, calls=%fused_computation.16 | convolution fusion | flops 5911347200 | bytes 21495808 | tf_op jit(solution)/shard_map/secd,edf->secf/dot_general | solution.py:8
  65.3 15.9 %fusion.12 = bf16[32,2,16,1408]{3,0,2,1:T(8,128)(2,1)S(1)} fusion(f32[32,2,16,1408]{3,0,2,1:T(8,128)} %bitcast_multiply_fusion.1, bf16[2,2048,1408]{2,1,0:T(8,128)(2,1)} %param.22, bf16[32,2,16,2048]{3,2,1,0:T(8,128)(2,1)} %param.17), kind=kOutput, calls=%fused_computation.15 | convolution fusion | flops 5908463616 | bytes 24379392 | tf_op jit(solution)/shard_map/secd,edf->secf/dot_general | solution.py:9
  81.2 9.7 %convert_bitcast_fusion = bf16[32,2,16,2048]{3,2,0,1:T(8,128)(2,1)S(1)} fusion(bf16[2,1408,2048]{2,1,0:T(8,128)(2,1)} %param.23, bf16[32,2,16,1408]{3,0,2,1:T(8,128)(2,1)S(1)} %fusion.12), kind=kOutput, calls=%fused_computation.29 | convolution fusion | flops 5907677184 | bytes 18612224 | tf_op jit(solution)/shard_map/secf,efd->secd/dot_general | solution.py:11
  90.9 2.5 %copy.45 = bf16[32,2,16,2048]{3,2,1,0:T(8,128)(2,1)} copy(bf16[32,2,16,2048]{3,2,0,1:T(8,128)(2,1)S(1)} %convert_bitcast_fusion) | data formatting | bytes 8388608 | tf_op jit(solution)/shard_map/convert_element_type | solution.py:11
  93.5 0.0 copy-start.2
  93.5 0.0 copy-start.3
  93.5 14.1 %all-to-all-done = bf16[32,2,16,2048]{3,2,1,0:T(8,128)(2,1)} async-done(((bf16[32,2,16,2048]{3,2,1,0:T(8,128)(2,1)}), bf16[32,2,16,2048]{3,2,1,0:T(8,128)(2,1)}, u32[]{:S(2)}, u32[]{:S(2)}) %all-to-all-start) | async-done | bytes 4194336 | tf_op jit(solution)/shard_map/all_to_all | solution.py:33
  107.6 3.8 %all-to-all-start.1 = ((bf16[32,2,16,2048]{3,2,1,0:T(8,128)(2,1)}), bf16[32,2,16,2048]{3,2,1,0:T(8,128)(2,1)}, u32[]{:S(2)}, u32[]{:S(2)}) async-start(bf16[32,2,16,2048]{3,2,1,0:T(8,128)(2,1)} %copy.45), calls=%async_computation.1 | async-start | bytes 8388608 | tf_op jit(solution)/shard_map/all_to_all | solution.py:33
  111.3 0.0 copy-done
  111.4 0.0 copy-done.4
  111.4 0.1 copy.39
  111.5 0.1 reshape.39
  111.6 0.0 copy-done.1
  111.6 0.0 copy-done.5
  111.7 0.1 copy.46
  111.7 0.1 reshape.43
  111.9 0.1 copy.34
  112.0 0.1 copy.41
  112.1 0.0 copy-done.2
  112.1 0.1 copy.33
  112.2 0.1 copy.40
  112.4 7.1 %gather_fusion = bf16[384,2048]{1,0:T(8,128)(2,1)S(1)} fusion(bf16[1024,2048]{1,0:T(8,128)(2,1)} %bitcast.9, s32[1024]{0:T(1024)S(1)} %pad_clamp_fusion.1), kind=kCustom, calls=%fused_computation.clone | custom fusion | bytes 3147264 | tf_op jit(solution)/shard_map/jit(_take)/gather | solution.py:18
  119.5 1.6 reshape.42
  121.1 47.4 %all-to-all-done.1 = bf16[32,2,16,2048]{3,2,1,0:T(8,128)(2,1)} async-done(((bf16[32,2,16,2048]{3,2,1,0:T(8,128)(2,1)}), bf16[32,2,16,2048]{3,2,1,0:T(8,128)(2,1)}, u32[]{:S(2)}, u32[]{:S(2)}) %all-to-all-start.1) | async-done | bytes 4194336 | tf_op jit(solution)/shard_map/all_to_all | solution.py:33
  168.5 7.1 %gather_fusion.1 = bf16[384,2048]{1,0:T(8,128)(2,1)S(1)} fusion(bf16[1024,2048]{1,0:T(8,128)(2,1)} %bitcast.16, s32[1024]{0:T(1024)S(1)} %pad_clamp_fusion), kind=kCustom, calls=%fused_computation.1.clone | custom fusion | bytes 3147264 | tf_op jit(solution)/shard_map/jit(_take)/gather | solution.py:18
  175.6 1.6 reshape.46
  177.3 6.7 %multiply_reduce_fusion = (bf16[64,2048]{1,0:T(8,128)(2,1)}, bf16[64,2048]{1,0:T(8,128)(2,1)}) fusion(bf16[64,6,2048]{2,1,0:T(8,128)(2,1)} %reshape.46, f32[64,6]{1,0:T(8,128)S(1)} %copy.40, pred[64,6]{1,0:T(8,128)(4,1)S(1)} %copy.41, bf16[64,6,2048]{2,1,0:T(8,128)(2,1)} %reshape.42, pred[64,6]{1,0:T(8,128)(4,1)S(1)} %copy.34, f32[64,6]{1,0:T(8,128)S(1)} %copy.33), kind=kLoop, calls=%fused_computation.28 | loop fusion | flops 6029312 | bytes 3673856 | tf_op jit(solution)/shard_map/reduce_sum | solution.py:20
  (11 shorter events, 0.0 us)
Async XLA Ops:
  43.0 64.6 %all-to-all-start = ((bf16[32,2,16,2048]{3,2,1,0:T(8,128)(2,1)}), bf16[32,2,16,2048]{3,2,1,0:T(8,128)(2,1)}, u32[]{:S(2)}, u32[]{:S(2)}) async-start(bf16[32,2,16,2048]{3,2,1,0:T(8,128)(2,1)} %copy.38), calls=%async_computation | async-start | bytes 8388608 | tf_op jit(solution)/shard_map/all_to_all | solution.py:33
  93.5 17.9 %copy-start = (s32[64,6]{0,1:T(8,128)S(1)}, s32[64,6]{0,1:T(8,128)}, u32[]{:S(2)}) copy-start(s32[64,6]{0,1:T(8,128)} %param.14) | copy-start | bytes 4612
  93.5 17.9 %copy-start.4 = (s32[64,6]{0,1:T(8,128)S(1)}, s32[64,6]{0,1:T(8,128)}, u32[]{:S(2)}) copy-start(s32[64,6]{0,1:T(8,128)} %param.15) | copy-start | bytes 4612
  93.5 18.1 %copy-start.1 = (s32[64,6]{0,1:T(8,128)S(1)}, s32[64,6]{0,1:T(8,128)}, u32[]{:S(2)}) copy-start(s32[64,6]{0,1:T(8,128)} %param.18) | copy-start | bytes 4612
  93.5 18.1 %copy-start.5 = (s32[64,6]{0,1:T(8,128)S(1)}, s32[64,6]{0,1:T(8,128)}, u32[]{:S(2)}) copy-start(s32[64,6]{0,1:T(8,128)} %param.19) | copy-start | bytes 4612
  93.5 18.6 %copy-start.2 = (f32[64,6]{0,1:T(8,128)S(1)}, f32[64,6]{0,1:T(8,128)}, u32[]{:S(2)}) copy-start(f32[64,6]{0,1:T(8,128)} %param.16) | copy-start | bytes 4612
  93.5 18.7 %copy-start.3 = (f32[64,6]{0,1:T(8,128)S(1)}, f32[64,6]{0,1:T(8,128)}, u32[]{:S(2)}) copy-start(f32[64,6]{0,1:T(8,128)} %param.20) | copy-start | bytes 4612
  107.6 60.9 %all-to-all-start.1 = ((bf16[32,2,16,2048]{3,2,1,0:T(8,128)(2,1)}), bf16[32,2,16,2048]{3,2,1,0:T(8,128)(2,1)}, u32[]{:S(2)}, u32[]{:S(2)}) async-start(bf16[32,2,16,2048]{3,2,1,0:T(8,128)(2,1)} %copy.45), calls=%async_computation.1 | async-start | bytes 8388608 | tf_op jit(solution)/shard_map/all_to_all | solution.py:33
where the time goes:
time: 184 us
  matrix products  79.6 us (43%)
  waiting for transfers between devices  61.5 us (33%)
  local copies, waits for them, and re-layouts  23.6 us (13%)
  starting transfers between devices  11.8 us (6%)
  other arithmetic  6.69 us (4%)
    all_to_all x2, waiting for transfers between devices, local_step(): returned = lax.all_to_all(y_rows, 'expert', 0, 0, tiled=True)  61.5 us
    dot_general x2, matrix products, expert_ffn(): jnp.einsum('secd,edf->secf', dispatched, w_up, preferred_element_type=jnp...  31.6 us
    dot_general x2, matrix products, expert_ffn(): jnp.einsum('secd,edf->secf', dispatched, w_gate, preferred_element_type=j...  28.7 us
    dot_general x2, matrix products, expert_ffn(): jnp.einsum('secf,efd->secd', hidden, w_down, preferred_element_type=jnp.f...  19.3 us
    gather x4, local copies, waits for them, and re-layouts, combine_rows(): picked = jnp.take(row_table, row_index, axis=0)  17.5 us
    all_to_all x2, starting transfers between devices, local_step(): returned = lax.all_to_all(y_rows, 'expert', 0, 0, tiled=True)  11.8 us
    reduce_sum x1, other arithmetic, combine_rows(): return jnp.sum(kept[:, :, None] * picked, axis=1).astype(jnp.bfloat16)  6.65 us
    convert_element_type x2, local copies, waits for them, and re-layouts, expert_ffn(): jnp.einsum('secf,efd->secd', hidden, w_down, preferred_element_type=jnp.f...  5.19 us
  transfers between devices with their start and end apart: 2, of which 2 were waited for; matrix products, arithmetic and copies ran while one was open for 28% of the time, Pallas kernels for 0%

commit v1 on v0

v1 whole, which is shorter than its diff:
```python
import functools
import math

import jax
import jax.numpy as jnp
from jax import lax
from jax.experimental import pallas as pl
from jax.experimental.pallas import tpu as pltpu
from jax.sharding import PartitionSpec as P

MESH = pl.DeviceIdType.MESH
AXIS = 'expert'
CORES = 2
BF16_MAX = 3.3895313892515355e38
NT = 256
DN = 512


def moe_kernel(side, top_k, disp_one, disp_two, meta_one, meta_two, w_gate, w_up, w_down, out_one, out_two,
               wgu, wd, stage, recv, hid, meta, part, relay, final,
               x_sem, w_sem, d_sem, send_sem, recv_sem, meta_send, meta_recv,
               part_send, relay_recv, final_recv):
    n_exp, dim, ffn = w_gate.shape
    cap = disp_one.shape[-2]
    half = dim // 2
    tokens = out_one.shape[0]
    rows = 2 * side * CORES * cap
    group = side * CORES * n_exp * cap
    n_main = ffn // NT
    tail = ffn - n_main * NT
    metas, disps, outs = (meta_one, meta_two), (disp_one, disp_two), (out_one, out_two)

    me = lax.axis_index(AXIS)
    c = me % CORES
    x = (me // CORES) % side
    y = me // (CORES * side)

    def dev(yy, xx, cc):
        return {AXIS: ((yy % side) * side + (xx % side)) * CORES + cc % CORES}

    def along(m, first, step, dc):
        if (m == 0) == first:
            return dev(y, x + step, c + dc)
        return dev(y + step, x, c + dc)

    def rel(it):
        return (2 - it + (it // 2) * (2 * it - 1)) % side

    def load_rows(u, it, e):
        r = rel(it)
        pltpu.make_async_copy(disp_one.at[(y + r) % side, :, e], stage.at[u, 0], x_sem.at[u, 0]).start()
        for k in range(side):
            pltpu.make_async_copy(disp_two.at[k, pl.ds((x + r) % side * CORES, CORES), e],
                                  stage.at[u, 1, k * CORES:(k + 1) * CORES], x_sem.at[u, 1]).start()

    def wait_rows(u):
        for m in range(2):
            pltpu.make_async_copy(stage.at[u, m], stage.at[u, m], x_sem.at[u, m]).wait()

    def load_weights(e):
        for j in range(n_main):
            for k, w in enumerate((w_gate, w_up)):
                pltpu.make_async_copy(w.at[e, :, pl.ds(j * NT, NT)], wgu.at[e, :, pl.ds((2 * j + k) * NT, NT)],
                                      w_sem.at[e, 2 * j + k]).start()
        for k, w in enumerate((w_gate, w_up)):
            pltpu.make_async_copy(w.at[e, :, pl.ds(n_main * NT, tail)],
                                  wgu.at[e, :, pl.ds(2 * n_main * NT + k * tail, tail)],
                                  w_sem.at[e, 2 * n_main + k]).start()
        for j in range(dim // DN):
            pltpu.make_async_copy(w_down.at[e, :, pl.ds(j * DN, DN)], wd.at[e, :, pl.ds(j * DN, DN)],
                                  d_sem.at[e, j]).start()

    def wait_gu(e, j):
        width = NT if j < n_main else tail
        for k in range(2):
            ref = wgu.at[e, :, pl.ds(2 * j * NT + k * width, width)]
            pltpu.make_async_copy(ref, ref, w_sem.at[e, 2 * j + k]).wait()

    def wait_down(e, j):
        ref = wd.at[e, :, pl.ds(j * DN, DN)]
        pltpu.make_async_copy(ref, ref, d_sem.at[e, j]).wait()

    def unit(u, e, first):
        wait_rows(u)
        for j in range(n_main + 1):
            width = NT if j < n_main else tail
            if first:
                wait_gu(e, j)
            both = jnp.dot(stage[u].reshape(rows, dim), wgu[e, :, 2 * j * NT:2 * j * NT + 2 * width],
                           preferred_element_type=jnp.float32)
            gate_act, up_act = both[:, :width], both[:, width:]
            hid[:, j * NT:j * NT + width] = (gate_act * jax.nn.sigmoid(gate_act) * up_act).astype(jnp.bfloat16)
        for j in range(dim // DN):
            if first:
                wait_down(e, j)
            y_rows = jnp.dot(hid[...], wd[e, :, j * DN:(j + 1) * DN], preferred_element_type=jnp.float32)
            y_rows = jnp.where(jnp.abs(y_rows) <= BF16_MAX, y_rows, 0.0).astype(jnp.bfloat16)
            stage[u, :, :, :, j * DN:(j + 1) * DN] = y_rows.reshape(2, side * CORES, cap, DN)

    hops = [(2, 0), (2, 1), (1, 0), (side - 1, 0), (1, 1), (side - 1, 1), (0, 1)]

    def send_unit(u, it, e):
        for step, dc in hops:
            for m in range(2):
                pos = x if m == 0 else y
                pltpu.make_async_remote_copy(
                    src_ref=stage.at[u, m, (pos + step) % side * CORES + (c + dc) % CORES],
                    dst_ref=recv.at[m, it, pos, c, e],
                    send_sem=send_sem.at[u, m], recv_sem=recv_sem.at[m, it],
                    device_id=along(m, True, step, dc), device_id_type=MESH).start()
        for m in range(2):
            pos = x if m == 0 else y
            pltpu.make_async_copy(stage.at[u, m, pos * CORES + c], recv.at[m, it, pos, c, e], recv_sem.at[m, it]).start()

    def combine(m, it, meta_tile):
        ref = recv.at[m, it]
        pltpu.make_async_copy(ref, ref, recv_sem.at[m, it]).wait()
        lane = lax.broadcasted_iota(jnp.int32, (tokens, group), 1)
        if m == 0:
            row_id = lane + y * group
        else:
            sub = CORES * n_exp * cap
            row_id = (lane // sub) * group + x * sub + lane % sub
        row_id = row_id.astype(jnp.float32)
        mix = jnp.zeros((tokens, group), jnp.float32)
        for j in range(top_k):
            mix = jnp.where(meta_tile[:, j:j + 1] == row_id, meta_tile[:, top_k + j:top_k + j + 1], mix)
        high = mix.astype(jnp.bfloat16)
        rest = mix - high.astype(jnp.float32)
        mid = rest.astype(jnp.bfloat16)
        low = (rest - mid.astype(jnp.float32)).astype(jnp.bfloat16)
        mix3 = jnp.concatenate([high, mid, low], axis=0)
        for j in range(dim // DN):
            table = recv[m, it, :, :, :, :, j * DN:(j + 1) * DN].reshape(group, DN)
            prod = jnp.dot(mix3, table, preferred_element_type=jnp.float32)
            total = prod[2 * tokens:] + prod[tokens:2 * tokens] + prod[:tokens]
            h, off = (j * DN) // half, (j * DN) % half
            part[m, it, h, :, off:off + DN] = total

    def wait_meta(m, it):
        ref = meta.at[m, it]
        pltpu.make_async_copy(ref, ref, meta_recv.at[m, it]).wait()

    load_rows(0, 0, 0)
    load_weights(0)
    load_rows(1, 0, 1)
    load_weights(1)

    barrier = pltpu.get_barrier_semaphore()
    peers = 0
    for step in range(side):
        for dc in range(CORES):
            if (step, dc) != (0, 0):
                pl.semaphore_signal(barrier, inc=1, device_id=along(0, True, step, dc), device_id_type=MESH)
                peers += 1
            if step != 0:
                pl.semaphore_signal(barrier, inc=1, device_id=along(1, True, step, dc), device_id_type=MESH)
                peers += 1

    def load_rest(u, carry):
        load_rows(u, u // n_exp, u % n_exp)
        return carry

    lax.fori_loop(n_exp, side * n_exp, load_rest, 0)
    pl.semaphore_wait(barrier, peers)

    for m in range(2):
        for it in range(side - 1):
            step = side - (2, 1, 3)[it]
            pltpu.make_async_remote_copy(src_ref=metas[m], dst_ref=meta.at[m, it], send_sem=meta_send.at[m, it],
                                         recv_sem=meta_recv.at[m, it], device_id=along(m, False, step, 0),
                                         device_id_type=MESH).start()

    for e in range(n_exp):
        unit(e, e, True)
        send_unit(e, 0, e)

    def send_far(m):
        for h, step in ((0, 1), (1, side - 1)):
            pltpu.make_async_remote_copy(src_ref=part.at[m, 0, h], dst_ref=relay.at[m, h],
                                         send_sem=part_send.at[m, h], recv_sem=relay_recv.at[m, h],
                                         device_id=along(m, False, step, 0), device_id_type=MESH).start()

    def body(it, carry):
        for e in range(n_exp):
            u = it * n_exp + e
            unit(u, e, False)
            send_unit(u, it, e)

        @pl.when(it < side - 1)
        def _():
            for m in range(2):
                @pl.when(it == 1)
                def _():
                    wait_meta(m, 0)

                @pl.when(it == 2)
                def _():
                    wait_meta(m, 1)
                combine(m, it - 1, meta[m, it - 1])

            @pl.when(it == 1)
            def _():
                for m in range(2):
                    send_far(m)
        return carry

    lax.fori_loop(1, side, body, 0)

    def send_near(m, it):
        h = it - 1
        step = (1, side - 1)[h]
        ref = relay.at[m, h]
        pltpu.make_async_copy(ref, ref, relay_recv.at[m, h]).wait()
        part[m, it, h] = part[m, it, h] + relay[m, h]
        pltpu.make_async_remote_copy(src_ref=part.at[m, it], dst_ref=final.at[m, h],
                                     send_sem=part_send.at[m, 2 + h], recv_sem=final_recv.at[m, h],
                                     device_id=along(m, False, step, 0), device_id_type=MESH).start()

    for m in range(2):
        send_near(m, 1)
    for m in range(2):
        wait_meta(m, 2)
        combine(m, 2, meta[m, 2])
        send_near(m, 2)
    for m in range(2):
        combine(m, 3, metas[m][...])
    for m in range(2):
        for h in range(2):
            ref = final.at[m, h]
            pltpu.make_async_copy(ref, ref, final_recv.at[m, h]).wait()
        for h in range(2):
            total = part[m, 3, h] + final[m, 0, h] + final[m, 1, h]
            outs[m][:, h * half:(h + 1) * half] = total.astype(jnp.bfloat16)

    def drain(u, carry):
        for m in range(2):
            ref = stage.at[u, m, pl.ds(0, side * CORES - 1)]
            pltpu.make_async_copy(ref, ref, send_sem.at[u, m]).wait()
        return carry

    lax.fori_loop(0, side * n_exp, drain, 0)
    for m in range(2):
        for it in range(side - 1):
            pltpu.make_async_copy(metas[m], metas[m], meta_send.at[m, it]).wait()
        for h in range(2):
            ref = part.at[m, 0, h]
            pltpu.make_async_copy(ref, ref, part_send.at[m, h]).wait()
            ref = part.at[m, 1 + h]
            pltpu.make_async_copy(ref, ref, part_send.at[m, 2 + h]).wait()


def solution(mesh):
    members = mesh.shape[AXIS]
    side = math.isqrt(members // CORES)
    disp_spec = P('data', 'expert', None, None)
    tok_spec = P(('data', 'expert'), None)
    weight_spec = P('expert', None, None)

    def local_step(disp_one, slot_one, expert_one, gate_one, disp_two, slot_two, expert_two, gate_two, w_gate, w_up, w_down):
        _, n_exp, cap, dim = disp_one.shape
        tokens, top_k = slot_one.shape
        ffn = w_gate.shape[-1]
        units = side * n_exp

        def pack(slot_ids, expert_ids, gates):
            rows = jnp.where(slot_ids >= 0, expert_ids * cap + slot_ids, -1).astype(jnp.float32)
            return jnp.pad(jnp.concatenate([rows, gates], axis=1), ((0, 0), (0, 128 - 2 * top_k)))

        split = (side, side * CORES, n_exp, cap, dim)
        any_spec = pl.BlockSpec(memory_space=pl.ANY)
        vmem_spec = pl.BlockSpec(memory_space=pltpu.VMEM)
        dma = pltpu.SemaphoreType.DMA
        flops = 2 * 2 * members * n_exp * cap * dim * ffn * 3
        return pl.pallas_call(
            functools.partial(moe_kernel, side, top_k),
            out_shape=(jax.ShapeDtypeStruct((tokens, dim), jnp.bfloat16),) * 2,
            in_specs=[any_spec, any_spec, vmem_spec, vmem_spec, any_spec, any_spec, any_spec],
            out_specs=(vmem_spec, vmem_spec),
            scratch_shapes=[
                pltpu.VMEM((n_exp, dim, 2 * ffn), jnp.bfloat16),
                pltpu.VMEM((n_exp, ffn, dim), jnp.bfloat16),
                pltpu.VMEM((units, 2, side * CORES, cap, dim), jnp.bfloat16),
                pltpu.VMEM((2, side, side, CORES, n_exp, cap, dim), jnp.bfloat16),
                pltpu.VMEM((2 * side * CORES * cap, ffn), jnp.bfloat16),
                pltpu.VMEM((2, side - 1, tokens, 128), jnp.float32),
                pltpu.VMEM((2, side, 2, tokens, dim // 2), jnp.float32),
                pltpu.VMEM((2, 2, tokens, dim // 2), jnp.float32),
                pltpu.VMEM((2, 2, 2, tokens, dim // 2), jnp.float32),
                dma((units, 2)), dma((n_exp, 2 * (ffn // NT) + 2)), dma((n_exp, dim // DN)),
                dma((units, 2)), dma((2, side)), dma((2, side - 1)), dma((2, side - 1)),
                dma((2, 4)), dma((2, 2)), dma((2, 2)),
            ],
            compiler_params=pltpu.CompilerParams(collective_id=0, has_side_effects=True,
                                                 vmem_limit_bytes=67_043_328),
            cost_estimate=pl.CostEstimate(flops=flops, bytes_accessed=43_000_000, transcendentals=0),
        )(disp_one.reshape(split), disp_two.reshape(split), pack(slot_one, expert_one, gate_one),
          pack(slot_two, expert_two, gate_two), w_gate, w_up, w_down)

    in_specs = (disp_spec, tok_spec, tok_spec, tok_spec, disp_spec, tok_spec, tok_spec, tok_spec,
                weight_spec, weight_spec, weight_spec)
    return jax.shard_map(local_step, mesh=mesh, in_specs=in_specs, out_specs=(tok_spec, tok_spec), check_vma=False)
```

time: 184 us -> 95.1 us (0.52)
  the two profiles are of different devices: /device:TPU:103 before, /device:TPU:97 now
where the time goes in v1:
time: 95.1 us; the launch traced here: 94.7 us
  Pallas kernels  86.5 us (91%)
  local copies, waits for them, and re-layouts  4.77 us (5%)
  other arithmetic  2.81 us (3%)
    pallas_call x1, Pallas kernels, local_step(): pl.pallas_call(functools.partial(moe_kernel, side, top_k), out_shape=(jax...  86.5 us
    unnamed x2, local copies, waits for them, and re-layouts  3.34 us

profile of v1, /device:TPU:97, one launch (start us, length us, event | category | flops | bytes accessed | tf_op | source)
XLA Modules:
  0.0 94.7 jit_solution(4596627024348118192)
XLA Ops:
  0.6 0.7 select_convert_fusion.1
  1.3 0.7 pad_maximum_fusion
  2.0 0.7 select_convert_fusion
  2.7 0.7 pad_maximum_fusion.1
  3.4 0.1 copy.26
  3.5 0.6 pad.8.meta_two
  4.2 0.1 copy.25
  4.2 0.6 pad.7.meta_one
  4.9 86.5 %shard_map.122 = (bf16[64,2048]{1,0:T(8,128)(2,1)}, bf16[64,2048]{1,0:T(8,128)(2,1)}) custom-call(bf16[4,8,2,16,2048]{4,3,2,1,0:T(8,128)(2,1)} %bitcast.2, bf16[4,8,2,16,2048]{4,3,2,1,0:T(8,128)(2,1)} %bitcast.3, f32[64,128]{1,0:T(8,128)} %pad.7.meta_one, f32[64,128]{1,0:T(8,128)} %pad.8.meta_two, bf16[2,2048,1408]{2,1,0:T(8,128)(2,1)} %w_gate.1, ...), custom_call_target="tpu_custom_call" | custom-call | flops 35433480192 | bytes 43000000 | tf_op jit(solution)/shard_map/pallas_call | solution.py:275
  91.4 1.7 %copy.29 = bf16[64,2048]{1,0:T(8,128)(2,1)} copy(bf16[64,2048]{1,0:T(8,128)(2,1)} %get-tuple-element.4) | data formatting | bytes 524288
  93.0 1.7 %copy.30 = bf16[64,2048]{1,0:T(8,128)(2,1)} copy(bf16[64,2048]{1,0:T(8,128)(2,1)} %get-tuple-element.5) | data formatting | bytes 524288

commit v2 on v1

v2 whole, which is shorter than its diff:
```python
import functools
import math

import jax
import jax.numpy as jnp
from jax import lax
from jax.experimental import pallas as pl
from jax.experimental.pallas import tpu as pltpu
from jax.sharding import PartitionSpec as P

MESH = pl.DeviceIdType.MESH
AXIS = 'expert'
CORES = 2
BF16_MAX = 3.3895313892515355e38
NT = 512
DN = 512
LANES = 128


def moe_kernel(side, disp_one, disp_two, slot_one, slot_two, expert_one, expert_two, gate_one, gate_two, w_gate, w_up, w_down, out_one, out_two,
               wgu, wd, stage, recv, hid, own, meta, part, relay, final,
               x_sem, w_sem, d_sem, send_sem, recv_sem, meta_send, meta_recv,
               part_send, relay_recv, final_recv):
    n_exp, dim, ffn = w_gate.shape
    cap = disp_one.shape[-2]
    half = dim // 2
    tokens = out_one.shape[0]
    rows = 2 * side * CORES * cap
    group = side * CORES * n_exp * cap
    n_main = ffn // NT
    tail = ffn - n_main * NT
    routes = ((slot_one, expert_one, gate_one), (slot_two, expert_two, gate_two))
    outs = (out_one, out_two)
    top_k = slot_one.shape[0]
    top_row = 8

    me = lax.axis_index(AXIS)
    c = me % CORES
    x = (me // CORES) % side
    y = me // (CORES * side)
    turn = 1 - 2 * c

    def dev(yy, xx, cc):
        return {AXIS: ((yy % side) * side + (xx % side)) * CORES + cc % CORES}

    def along(m, first, step, dc):
        if (m == 0) == first:
            return dev(y, x + step, c + dc)
        return dev(y + step, x, c + dc)

    def rel(it):
        return (2 - it + (it // 2) * (2 * it - 1)) % side

    def load_rows(u, it, e):
        for k in range(CORES):
            r = (1 - 2 * k) * rel(it) + side
            pltpu.make_async_copy(disp_one.at[(y + r) % side, :, k, e], stage.at[u, 0, pl.ds(k * side, side)], x_sem.at[u, 0]).start()
            pltpu.make_async_copy(disp_two.at[:, (x + r) % side, k, e], stage.at[u, 1, pl.ds(k * side, side)], x_sem.at[u, 1]).start()

    def wait_rows(u):
        for m in range(2):
            pltpu.make_async_copy(stage.at[u, m], stage.at[u, m], x_sem.at[u, m]).wait()

    def load_weights(e):
        for j in range(n_main):
            for k, w in enumerate((w_gate, w_up)):
                pltpu.make_async_copy(w.at[e, :, pl.ds(j * NT, NT)], wgu.at[e, :, pl.ds((2 * j + k) * NT, NT)],
                                      w_sem.at[e, 2 * j + k]).start()
        for k, w in enumerate((w_gate, w_up)):
            pltpu.make_async_copy(w.at[e, :, pl.ds(n_main * NT, tail)],
                                  wgu.at[e, :, pl.ds(2 * n_main * NT + k * tail, tail)],
                                  w_sem.at[e, 2 * n_main + k]).start()
        for j in range(dim // DN):
            pltpu.make_async_copy(w_down.at[e, :, pl.ds(j * DN, DN)], wd.at[e, :, pl.ds(j * DN, DN)],
                                  d_sem.at[e, j]).start()

    def wait_gu(e, j):
        width = NT if j < n_main else tail
        for k in range(2):
            ref = wgu.at[e, :, pl.ds(2 * j * NT + k * width, width)]
            pltpu.make_async_copy(ref, ref, w_sem.at[e, 2 * j + k]).wait()

    def wait_down(e, j):
        ref = wd.at[e, :, pl.ds(j * DN, DN)]
        pltpu.make_async_copy(ref, ref, d_sem.at[e, j]).wait()

    def hidden(j, both):
        width = NT if j < n_main else tail
        gate_act, up_act = both[:, :width], both[:, width:]
        hid[:, j * NT:j * NT + width] = (gate_act * jax.nn.sigmoid(gate_act) * up_act).astype(jnp.bfloat16)

    def put_rows(u, j, width, y_rows):
        y_rows = jnp.where(jnp.abs(y_rows) <= BF16_MAX, y_rows, 0.0).astype(jnp.bfloat16)
        stage[u, :, :, :, j * width:(j + 1) * width] = y_rows.reshape(2, CORES * side, cap, width)

    def dot(a, b):
        return jnp.dot(a, b, preferred_element_type=jnp.float32)

    def first_unit(u, e):
        wait_rows(u)
        for j in range(n_main + 1):
            width = NT if j < n_main else tail
            wait_gu(e, j)
            hidden(j, dot(stage[u].reshape(rows, dim), wgu[e, :, 2 * j * NT:2 * j * NT + 2 * width]))
        for j in range(dim // DN):
            wait_down(e, j)
            put_rows(u, j, DN, dot(hid[...], wd[e, :, j * DN:(j + 1) * DN]))

    def unit(u, e):
        wait_rows(u)
        both = dot(stage[u].reshape(rows, dim), wgu[e])
        for j in range(n_main + 1):
            width = NT if j < n_main else tail
            hidden(j, both[:, 2 * j * NT:2 * j * NT + 2 * width])
        put_rows(u, 0, dim, dot(hid[...], wd[e]))

    hops = [(2, 0), (2, 1), (1, 0), (side - 1, 0), (1, 1), (side - 1, 1), (0, 1)]

    def send_unit(u, it, e):
        for step, dc in hops:
            for m in range(2):
                pos = x if m == 0 else y
                pltpu.make_async_remote_copy(
                    src_ref=stage.at[u, m, (c + dc) % CORES * side + (pos + step) % side],
                    dst_ref=recv.at[m, it, pos, c, e],
                    send_sem=send_sem.at[u, m], recv_sem=recv_sem.at[m, it],
                    device_id=along(m, True, step, dc), device_id_type=MESH).start()
        for m in range(2):
            pos = x if m == 0 else y
            pltpu.make_async_copy(stage.at[u, m, c * side + pos], recv.at[m, it, pos, c, e], recv_sem.at[m, it]).start()

    def combine(m, it, meta_tile):
        ref = recv.at[m, it]
        pltpu.make_async_copy(ref, ref, recv_sem.at[m, it]).wait()
        lane = lax.broadcasted_iota(jnp.int32, (tokens, group), 1)
        if m == 0:
            row_id = lane + y * group
        else:
            sub = CORES * n_exp * cap
            row_id = (lane // sub) * group + x * sub + lane % sub
        row_id = row_id.astype(jnp.float32)
        table = jnp.transpose(meta_tile)
        mix = jnp.zeros((tokens, group), jnp.float32)
        for j in range(top_k):
            mix = jnp.where(table[:tokens, j:j + 1] == row_id, table[:tokens, top_row + j:top_row + j + 1], mix)
        high = mix.astype(jnp.bfloat16)
        rest = mix - high.astype(jnp.float32)
        mid = rest.astype(jnp.bfloat16)
        low = (rest - mid.astype(jnp.float32)).astype(jnp.bfloat16)
        mix3 = jnp.concatenate([high, mid, low], axis=0)
        for j in range(dim // DN):
            prod = dot(mix3, recv[m, it, :, :, :, :, j * DN:(j + 1) * DN].reshape(group, DN))
            total = prod[2 * tokens:] + prod[tokens:2 * tokens] + prod[:tokens]
            h, off = (j * DN) // half, (j * DN) % half
            part[m, it, h, :, off:off + DN] = total

    def wait_meta(m, it):
        ref = meta.at[m, it]
        pltpu.make_async_copy(ref, ref, meta_recv.at[m, it]).wait()

    load_rows(0, 0, 0)
    load_weights(0)
    load_rows(1, 0, 1)
    load_weights(1)

    barrier = pltpu.get_barrier_semaphore()
    peers = 0
    for step in range(side):
        for dc in range(CORES):
            if (step, dc) != (0, 0):
                pl.semaphore_signal(barrier, inc=1, device_id=along(0, True, step, dc), device_id_type=MESH)
                peers += 1
            if step != 0:
                pl.semaphore_signal(barrier, inc=1, device_id=along(1, True, step, dc), device_id_type=MESH)
                peers += 1

    def load_rest(u, carry):
        load_rows(u, u // n_exp, u % n_exp)
        return carry

    lax.fori_loop(n_exp, side * n_exp, load_rest, 0)
    for m, (slots, experts, gates) in enumerate(routes):
        own[m] = jnp.zeros((2 * top_row, LANES), jnp.float32)
        kept = slots[...] >= 0
        own[m, :top_k, :tokens] = jnp.where(kept, experts[...] * cap + slots[...], -1).astype(jnp.float32)
        own[m, top_row:top_row + top_k, :tokens] = gates[...]
    pl.semaphore_wait(barrier, peers)

    for m in range(2):
        for it in range(side - 1):
            step = side - turn * (2, 1, 3)[it]
            pltpu.make_async_remote_copy(src_ref=own.at[m], dst_ref=meta.at[m, it], send_sem=meta_send.at[m, it],
                                         recv_sem=meta_recv.at[m, it], device_id=along(m, False, step, 0),
                                         device_id_type=MESH).start()

    for e in range(n_exp):
        first_unit(e, e)
        send_unit(e, 0, e)

    def send_far(m):
        for h, step in ((0, side + turn), (1, side - turn)):
            pltpu.make_async_remote_copy(src_ref=part.at[m, 0, h], dst_ref=relay.at[m, h],
                                         send_sem=part_send.at[m, h], recv_sem=relay_recv.at[m, h],
                                         device_id=along(m, False, step, 0), device_id_type=MESH).start()

    def send_near(m, it):
        h = it - 1
        step = side + (turn, -turn)[h]
        ref = relay.at[m, h]
        pltpu.make_async_copy(ref, ref, relay_recv.at[m, h]).wait()
        part[m, it, h] = part[m, it, h] + relay[m, h]
        pltpu.make_async_remote_copy(src_ref=part.at[m, it], dst_ref=final.at[m, h],
                                     send_sem=part_send.at[m, 2 + h], recv_sem=final_recv.at[m, h],
                                     device_id=along(m, False, step, 0), device_id_type=MESH).start()

    def body(it, carry):
        for e in range(n_exp):
            u = it * n_exp + e
            unit(u, e)
            send_unit(u, it, e)

        @pl.when(it < side - 1)
        def _():
            for m in range(2):
                @pl.when(it == 1)
                def _():
                    wait_meta(m, 0)

                @pl.when(it == 2)
                def _():
                    wait_meta(m, 1)
                combine(m, it - 1, meta[m, it - 1])

            @pl.when(it == 1)
            def _():
                for m in range(2):
                    send_far(m)

            @pl.when(it == 2)
            def _():
                for m in range(2):
                    send_near(m, 1)
        return carry

    lax.fori_loop(1, side, body, 0)
    for m in range(2):
        wait_meta(m, 2)
        combine(m, 2, meta[m, 2])
        send_near(m, 2)
    for m in range(2):
        combine(m, 3, own[m])
    for m in range(2):
        for h in range(2):
            ref = final.at[m, h]
            pltpu.make_async_copy(ref, ref, final_recv.at[m, h]).wait()
        for h in range(2):
            total = part[m, 3, h] + final[m, 0, h] + final[m, 1, h]
            outs[m][:, h * half:(h + 1) * half] = total.astype(jnp.bfloat16)

    def drain(u, carry):
        for m in range(2):
            ref = stage.at[u, m, pl.ds(0, side * CORES - 1)]
            pltpu.make_async_copy(ref, ref, send_sem.at[u, m]).wait()
        return carry

    lax.fori_loop(0, side * n_exp, drain, 0)
    for m in range(2):
        for it in range(side - 1):
            pltpu.make_async_copy(own.at[m], own.at[m], meta_send.at[m, it]).wait()
        for h in range(2):
            ref = part.at[m, 0, h]
            pltpu.make_async_copy(ref, ref, part_send.at[m, h]).wait()
            ref = part.at[m, 1 + h]
            pltpu.make_async_copy(ref, ref, part_send.at[m, 2 + h]).wait()


def solution(mesh):
    members = mesh.shape[AXIS]
    side = math.isqrt(members // CORES)
    disp_spec = P('data', 'expert', None, None)
    tok_spec = P(('data', 'expert'), None)
    weight_spec = P('expert', None, None)

    def local_step(disp_one, slot_one, expert_one, gate_one, disp_two, slot_two, expert_two, gate_two, w_gate, w_up, w_down):
        _, n_exp, cap, dim = disp_one.shape
        tokens = slot_one.shape[0]
        ffn = w_gate.shape[-1]
        units = side * n_exp

        split = (side, side, CORES, n_exp, cap, dim)
        any_spec = pl.BlockSpec(memory_space=pl.ANY)
        vmem_spec = pl.BlockSpec(memory_space=pltpu.VMEM)
        dma = pltpu.SemaphoreType.DMA
        flops = 2 * 2 * members * n_exp * cap * dim * ffn * 3
        return pl.pallas_call(
            functools.partial(moe_kernel, side),
            out_shape=(jax.ShapeDtypeStruct((tokens, dim), jnp.bfloat16),) * 2,
            in_specs=[any_spec] * 2 + [vmem_spec] * 6 + [any_spec] * 3,
            out_specs=(vmem_spec, vmem_spec),
            scratch_shapes=[
                pltpu.VMEM((n_exp, dim, 2 * ffn), jnp.bfloat16),
                pltpu.VMEM((n_exp, ffn, dim), jnp.bfloat16),
                pltpu.VMEM((units, 2, CORES * side, cap, dim), jnp.bfloat16),
                pltpu.VMEM((2, side, side, CORES, n_exp, cap, dim), jnp.bfloat16),
                pltpu.VMEM((2 * side * CORES * cap, ffn), jnp.bfloat16),
                pltpu.VMEM((2, 16, LANES), jnp.float32),
                pltpu.VMEM((2, side - 1, 16, LANES), jnp.float32),
                pltpu.VMEM((2, side, 2, tokens, dim // 2), jnp.float32),
                pltpu.VMEM((2, 2, tokens, dim // 2), jnp.float32),
                pltpu.VMEM((2, 2, 2, tokens, dim // 2), jnp.float32),
                dma((units, 2)), dma((n_exp, 2 * (ffn // NT) + 2)), dma((n_exp, dim // DN)),
                dma((units, 2)), dma((2, side)), dma((2, side - 1)), dma((2, side - 1)),
                dma((2, 4)), dma((2, 2)), dma((2, 2)),
            ],
            compiler_params=pltpu.CompilerParams(collective_id=0, has_side_effects=True,
                                                 vmem_limit_bytes=67_043_328),
            cost_estimate=pl.CostEstimate(flops=flops, bytes_accessed=43_000_000, transcendentals=0),
        )(disp_one.reshape(split), disp_two.reshape(split), slot_one.T, slot_two.T, expert_one.T, expert_two.T,
          gate_one.T, gate_two.T, w_gate, w_up, w_down)

    in_specs = (disp_spec, tok_spec, tok_spec, tok_spec, disp_spec, tok_spec, tok_spec, tok_spec,
                weight_spec, weight_spec, weight_spec)
    return jax.shard_map(local_step, mesh=mesh, in_specs=in_specs, out_specs=(tok_spec, tok_spec), check_vma=False)
```

time: 95.1 us -> 89.1 us (0.937)
  other arithmetic: 2.81 us -> 0 us
  Pallas kernels: 86.5 us -> 84.9 us
  local copies, waits for them, and re-layouts: 4.77 us -> 3.34 us
    pallas_call x1, Pallas kernels: 86.5 us -> 84.9 us  [local_step(): pl.pallas_call(functools.partial(moe_kernel, side), out_shape=(jax.ShapeD...]
    convert_element_type x2 -> x0, other arithmetic: 1.42 us -> none  [pack(): jnp.where(slot_ids >= 0, expert_ids * cap + slot_ids, -1)]
    concatenate x2 -> x0, other arithmetic: 1.39 us -> none  [pack(): jnp.concatenate([rows, gates], axis=1)]
    pad x2 -> x0, local copies, waits for them, and re-layouts: 1.24 us -> none  [pack(): jnp.pad(jnp.concatenate([rows, gates], axis=1), ((0, 0), (0, 128 - 2 * to...]
where the time goes in v2:
time: 89.1 us; the launch traced here: 88.9 us
  Pallas kernels  84.9 us (95%)
  local copies, waits for them, and re-layouts  3.34 us (4%)
    pallas_call x1, Pallas kernels, local_step(): pl.pallas_call(functools.partial(moe_kernel, side), out_shape=(jax.ShapeD...  84.9 us
    unnamed x2, local copies, waits for them, and re-layouts  3.34 us

profile of v2, /device:TPU:97, one launch (start us, length us, event | category | flops | bytes accessed | tf_op | source)
XLA Modules:
  0.0 88.9 jit_solution(8234619625293411879)
XLA Ops:
  0.6 84.9 %shard_map.122 = (bf16[64,2048]{1,0:T(8,128)(2,1)}, bf16[64,2048]{1,0:T(8,128)(2,1)}) custom-call(bf16[4,4,2,2,16,2048]{5,4,3,2,1,0:T(8,128)(2,1)} %bitcast.8, bf16[4,4,2,2,16,2048]{5,4,3,2,1,0:T(8,128)(2,1)} %bitcast.9, s32[6,64]{1,0:T(8,128)} %bitcast.10, s32[6,64]{1,0:T(8,128)} %bitcast.11, s32[6,64]{1,0:T(8,128)} %bitcast.12, s32[6,64]{1,0:T(8,128)} %bitcast.13, ...), custom_call_target="tpu_custom_call" | custom-call | flops 35433480192 | bytes 43000000 | tf_op jit(solution)/shard_map/pallas_call | solution.py:295
  85.6 1.7 %copy.15 = bf16[64,2048]{1,0:T(8,128)(2,1)} copy(bf16[64,2048]{1,0:T(8,128)(2,1)} %get-tuple-element.4) | data formatting | bytes 524288
  87.2 1.7 %copy.16 = bf16[64,2048]{1,0:T(8,128)(2,1)} copy(bf16[64,2048]{1,0:T(8,128)(2,1)} %get-tuple-element.5) | data formatting | bytes 524288

commit v3 on v2

--- a/solution.py
+++ b/solution.py
@@ -13,7 +13,7 @@
 CORES = 2
 BF16_MAX = 3.3895313892515355e38
 NT = 512
-DN = 512
+DN = 1024
 LANES = 128
 
 
@@ -61,18 +61,30 @@
         for m in range(2):
             pltpu.make_async_copy(stage.at[u, m], stage.at[u, m], x_sem.at[u, m]).wait()
 
-    def load_weights(e):
-        for j in range(n_main):
-            for k, w in enumerate((w_gate, w_up)):
-                pltpu.make_async_copy(w.at[e, :, pl.ds(j * NT, NT)], wgu.at[e, :, pl.ds((2 * j + k) * NT, NT)],
-                                      w_sem.at[e, 2 * j + k]).start()
+    def load_gu(e, j, priority=0):
+        width = NT if j < n_main else tail
         for k, w in enumerate((w_gate, w_up)):
-            pltpu.make_async_copy(w.at[e, :, pl.ds(n_main * NT, tail)],
-                                  wgu.at[e, :, pl.ds(2 * n_main * NT + k * tail, tail)],
-                                  w_sem.at[e, 2 * n_main + k]).start()
-        for j in range(dim // DN):
-            pltpu.make_async_copy(w_down.at[e, :, pl.ds(j * DN, DN)], wd.at[e, :, pl.ds(j * DN, DN)],
-                                  d_sem.at[e, j]).start()
+            pltpu.make_async_copy(w.at[e, :, pl.ds(j * NT, width)],
+                                  wgu.at[e, :, pl.ds(2 * j * NT + k * width, width)],
+                                  w_sem.at[e, 2 * j + k]).start(priority=priority)
+
+    def load_down(e, j):
+        pltpu.make_async_copy(w_down.at[e, :, pl.ds(j * DN, DN)], wd.at[e, :, pl.ds(j * DN, DN)],
+                              d_sem.at[e, j]).start()
+
+    chunks = []
+    for e in range(n_exp):
+        chunks.append(lambda e=e: (load_rows(e, 0, e), load_gu(e, 0)))
+        chunks.extend(functools.partial(load_gu, e, j) for j in range(1, n_main + 1))
+        chunks.extend(functools.partial(load_down, e, j) for j in range(dim // DN))
+    for it in range(1, side):
+        chunks.append(lambda it=it: [load_rows(it * n_exp + e, it, e) for e in range(n_exp)])
+    chunks = iter(chunks)
+
+    def next_chunk():
+        for load in chunks:
+            load()
+            return
 
     def wait_gu(e, j):
         width = NT if j < n_main else tail
@@ -101,9 +113,11 @@
         for j in range(n_main + 1):
             width = NT if j < n_main else tail
             wait_gu(e, j)
+            next_chunk()
             hidden(j, dot(stage[u].reshape(rows, dim), wgu[e, :, 2 * j * NT:2 * j * NT + 2 * width]))
         for j in range(dim // DN):
             wait_down(e, j)
+            next_chunk()
             put_rows(u, j, DN, dot(hid[...], wd[e, :, j * DN:(j + 1) * DN]))
 
     def unit(u, e):
@@ -158,10 +172,8 @@
         ref = meta.at[m, it]
         pltpu.make_async_copy(ref, ref, meta_recv.at[m, it]).wait()
 
-    load_rows(0, 0, 0)
-    load_weights(0)
-    load_rows(1, 0, 1)
-    load_weights(1)
+    next_chunk()
+    next_chunk()
 
     barrier = pltpu.get_barrier_semaphore()
     peers = 0
@@ -174,18 +186,14 @@
                 pl.semaphore_signal(barrier, inc=1, device_id=along(1, True, step, dc), device_id_type=MESH)
                 peers += 1
 
-    def load_rest(u, carry):
-        load_rows(u, u // n_exp, u % n_exp)
-        return carry
-
-    lax.fori_loop(n_exp, side * n_exp, load_rest, 0)
     for m, (slots, experts, gates) in enumerate(routes):
         own[m] = jnp.zeros((2 * top_row, LANES), jnp.float32)
         kept = slots[...] >= 0
         own[m, :top_k, :tokens] = jnp.where(kept, experts[...] * cap + slots[...], -1).astype(jnp.float32)
         own[m, top_row:top_row + top_k, :tokens] = gates[...]
+    first_unit(0, 0)
     pl.semaphore_wait(barrier, peers)
-
+    send_unit(0, 0, 0)
     for m in range(2):
         for it in range(side - 1):
             step = side - turn * (2, 1, 3)[it]
@@ -193,9 +201,11 @@
                                          recv_sem=meta_recv.at[m, it], device_id=along(m, False, step, 0),
                                          device_id_type=MESH).start()
 
-    for e in range(n_exp):
+    for e in range(1, n_exp):
         first_unit(e, e)
         send_unit(e, 0, e)
+    for _ in range(side):
+        next_chunk()
 
     def send_far(m):
         for h, step in ((0, side + turn), (1, side - turn)):
@@ -274,6 +284,11 @@
             pltpu.make_async_copy(ref, ref, part_send.at[m, 2 + h]).wait()
 
 
+def copy_kernel(in_one, in_two, out_one, out_two):
+    out_one[...] = in_one[...]
+    out_two[...] = in_two[...]
+
+
 def solution(mesh):
     members = mesh.shape[AXIS]
     side = math.isqrt(members // CORES)
@@ -292,7 +307,7 @@
         vmem_spec = pl.BlockSpec(memory_space=pltpu.VMEM)
         dma = pltpu.SemaphoreType.DMA
         flops = 2 * 2 * members * n_exp * cap * dim * ffn * 3
-        return pl.pallas_call(
+        outs = pl.pallas_call(
             functools.partial(moe_kernel, side),
             out_shape=(jax.ShapeDtypeStruct((tokens, dim), jnp.bfloat16),) * 2,
             in_specs=[any_spec] * 2 + [vmem_spec] * 6 + [any_spec] * 3,
@@ -317,6 +332,9 @@
             cost_estimate=pl.CostEstimate(flops=flops, bytes_accessed=43_000_000, transcendentals=0),
         )(disp_one.reshape(split), disp_two.reshape(split), slot_one.T, slot_two.T, expert_one.T, expert_two.T,
           gate_one.T, gate_two.T, w_gate, w_up, w_down)
+        return pl.pallas_call(
+            copy_kernel, out_shape=(jax.ShapeDtypeStruct((tokens, dim), jnp.bfloat16),) * 2,
+            in_specs=[vmem_spec, vmem_spec], out_specs=(vmem_spec, vmem_spec))(*outs)
 
     in_specs = (disp_spec, tok_spec, tok_spec, tok_spec, disp_spec, tok_spec, tok_spec, tok_spec,
                 weight_spec, weight_spec, weight_spec)

time: 89.1 us -> 83.6 us (0.938)
  local copies, waits for them, and re-layouts: 3.34 us -> 0 us
  Pallas kernels: 84.9 us -> 82.8 us
    pallas_call x1, Pallas kernels: 84.9 us -> 81 us  [local_step(): pl.pallas_call(functools.partial(moe_kernel, side), out_shape=(jax.ShapeD...]
    unnamed x2 -> x0, local copies, waits for them, and re-layouts: 3.34 us -> none
    pallas_call x0 -> x1, Pallas kernels: none -> 1.84 us  [local_step(): pl.pallas_call(copy_kernel, out_shape=(jax.ShapeDtypeStruct((tokens, dim)...]
where the time goes in v3:
time: 83.6 us; the launch traced here: 83.4 us
  Pallas kernels  82.8 us (99%)
    pallas_call x1, Pallas kernels, local_step(): pl.pallas_call(functools.partial(moe_kernel, side), out_shape=(jax.ShapeD...  81 us
    pallas_call x1, Pallas kernels, local_step(): pl.pallas_call(copy_kernel, out_shape=(jax.ShapeDtypeStruct((tokens, dim)...  1.84 us

profile of v3, /device:TPU:97, one launch (start us, length us, event | category | flops | bytes accessed | tf_op | source)
XLA Modules:
  0.0 83.4 jit_solution(9301969002166857503)
XLA Ops:
  0.6 81.0 %shard_map.122 = (bf16[64,2048]{1,0:T(8,128)(2,1)}, bf16[64,2048]{1,0:T(8,128)(2,1)}) custom-call(bf16[4,4,2,2,16,2048]{5,4,3,2,1,0:T(8,128)(2,1)} %bitcast.8, bf16[4,4,2,2,16,2048]{5,4,3,2,1,0:T(8,128)(2,1)} %bitcast.9, s32[6,64]{1,0:T(8,128)} %bitcast.10, s32[6,64]{1,0:T(8,128)} %bitcast.11, s32[6,64]{1,0:T(8,128)} %bitcast.12, s32[6,64]{1,0:T(8,128)} %bitcast.13, ...), custom_call_target="tpu_custom_call" | custom-call | flops 35433480192 | bytes 43000000 | tf_op jit(solution)/shard_map/pallas_call | solution.py:310
  81.6 1.8 %shard_map.123 = (bf16[64,2048]{1,0:T(8,128)(2,1)}, bf16[64,2048]{1,0:T(8,128)(2,1)}) custom-call(bf16[64,2048]{1,0:T(8,128)(2,1)} %get-tuple-element.4.in_one, bf16[64,2048]{1,0:T(8,128)(2,1)} %get-tuple-element.5.in_two), custom_call_target="tpu_custom_call" | custom-call | tf_op jit(solution)/shard_map/pallas_call | solution.py:335

commit v4 on v3

--- a/solution.py
+++ b/solution.py
@@ -12,7 +12,9 @@
 AXIS = 'expert'
 CORES = 2
 BF16_MAX = 3.3895313892515355e38
-NT = 512
+TILES = (512, 512)
+PIECE = 512
+IN_FLIGHT = 9_500_000
 DN = 1024
 LANES = 128
 
@@ -27,8 +29,8 @@
     tokens = out_one.shape[0]
     rows = 2 * side * CORES * cap
     group = side * CORES * n_exp * cap
-    n_main = ffn // NT
-    tail = ffn - n_main * NT
+    widths = TILES + (ffn - sum(TILES),)
+    starts = [sum(widths[:j]) for j in range(len(widths))]
     routes = ((slot_one, expert_one, gate_one), (slot_two, expert_two, gate_two))
     outs = (out_one, out_two)
     top_k = slot_one.shape[0]
@@ -61,45 +63,52 @@
         for m in range(2):
             pltpu.make_async_copy(stage.at[u, m], stage.at[u, m], x_sem.at[u, m]).wait()
 
-    def load_gu(e, j, priority=0):
-        width = NT if j < n_main else tail
+    def load_gu(e, j, off, width):
         for k, w in enumerate((w_gate, w_up)):
-            pltpu.make_async_copy(w.at[e, :, pl.ds(j * NT, width)],
-                                  wgu.at[e, :, pl.ds(2 * j * NT + k * width, width)],
-                                  w_sem.at[e, 2 * j + k]).start(priority=priority)
+            pltpu.make_async_copy(w.at[e, :, pl.ds(starts[j] + off, width)],
+                                  wgu.at[e, :, pl.ds(2 * starts[j] + k * widths[j] + off, width)],
+                                  w_sem.at[e, j]).start()
 
     def load_down(e, j):
         pltpu.make_async_copy(w_down.at[e, :, pl.ds(j * DN, DN)], wd.at[e, :, pl.ds(j * DN, DN)],
                               d_sem.at[e, j]).start()
 
+    row_bytes = 2 * rows * dim
+    gu_bytes = lambda width: 2 * 2 * dim * width
+    down_bytes = 2 * ffn * DN
     chunks = []
     for e in range(n_exp):
-        chunks.append(lambda e=e: (load_rows(e, 0, e), load_gu(e, 0)))
-        chunks.extend(functools.partial(load_gu, e, j) for j in range(1, n_main + 1))
-        chunks.extend(functools.partial(load_down, e, j) for j in range(dim // DN))
+        chunks.append((row_bytes, functools.partial(load_rows, e, 0, e)))
+        for j, width in enumerate(widths):
+            for off in range(0, width, PIECE):
+                piece = min(PIECE, width - off)
+                chunks.append((gu_bytes(piece), functools.partial(load_gu, e, j, off, piece)))
+        for j in range(dim // DN):
+            chunks.append((down_bytes, functools.partial(load_down, e, j)))
     for it in range(1, side):
-        chunks.append(lambda it=it: [load_rows(it * n_exp + e, it, e) for e in range(n_exp)])
-    chunks = iter(chunks)
-
-    def next_chunk():
-        for load in chunks:
+        for e in range(n_exp):
+            chunks.append((row_bytes, functools.partial(load_rows, it * n_exp + e, it, e)))
+    flying = [0]
+
+    def next_chunks(done):
+        flying[0] -= done
+        while chunks and flying[0] + chunks[0][0] <= IN_FLIGHT:
+            size, load = chunks.pop(0)
+            flying[0] += size
             load()
-            return
 
     def wait_gu(e, j):
-        width = NT if j < n_main else tail
-        for k in range(2):
-            ref = wgu.at[e, :, pl.ds(2 * j * NT + k * width, width)]
-            pltpu.make_async_copy(ref, ref, w_sem.at[e, 2 * j + k]).wait()
+        ref = wgu.at[e, :, pl.ds(2 * starts[j], 2 * widths[j])]
+        pltpu.make_async_copy(ref, ref, w_sem.at[e, j]).wait()
 
     def wait_down(e, j):
         ref = wd.at[e, :, pl.ds(j * DN, DN)]
         pltpu.make_async_copy(ref, ref, d_sem.at[e, j]).wait()
 
     def hidden(j, both):
-        width = NT if j < n_main else tail
+        width = widths[j]
         gate_act, up_act = both[:, :width], both[:, width:]
-        hid[:, j * NT:j * NT + width] = (gate_act * jax.nn.sigmoid(gate_act) * up_act).astype(jnp.bfloat16)
+        hid[:, starts[j]:starts[j] + width] = (gate_act * jax.nn.sigmoid(gate_act) * up_act).astype(jnp.bfloat16)
 
     def put_rows(u, j, width, y_rows):
         y_rows = jnp.where(jnp.abs(y_rows) <= BF16_MAX, y_rows, 0.0).astype(jnp.bfloat16)
@@ -108,40 +117,43 @@
     def dot(a, b):
         return jnp.dot(a, b, preferred_element_type=jnp.float32)
 
-    def first_unit(u, e):
+    def first_unit(u, e, ready):
         wait_rows(u)
-        for j in range(n_main + 1):
-            width = NT if j < n_main else tail
+        done = row_bytes
+        for j, width in enumerate(widths):
             wait_gu(e, j)
-            next_chunk()
-            hidden(j, dot(stage[u].reshape(rows, dim), wgu[e, :, 2 * j * NT:2 * j * NT + 2 * width]))
+            next_chunks(done + gu_bytes(width))
+            done = 0
+            hidden(j, dot(stage[u].reshape(rows, dim), wgu[e, :, 2 * starts[j]:2 * starts[j] + 2 * width]))
         for j in range(dim // DN):
             wait_down(e, j)
-            next_chunk()
+            next_chunks(down_bytes)
             put_rows(u, j, DN, dot(hid[...], wd[e, :, j * DN:(j + 1) * DN]))
+        ready()
+        send_unit(u, 0, e)
 
     def unit(u, e):
         wait_rows(u)
         both = dot(stage[u].reshape(rows, dim), wgu[e])
-        for j in range(n_main + 1):
-            width = NT if j < n_main else tail
-            hidden(j, both[:, 2 * j * NT:2 * j * NT + 2 * width])
+        for j, width in enumerate(widths):
+            hidden(j, both[:, 2 * starts[j]:2 * starts[j] + 2 * width])
         put_rows(u, 0, dim, dot(hid[...], wd[e]))
 
     hops = [(2, 0), (2, 1), (1, 0), (side - 1, 0), (1, 1), (side - 1, 1), (0, 1)]
 
-    def send_unit(u, it, e):
+    def send_unit(u, it, e, cols=slice(None)):
         for step, dc in hops:
             for m in range(2):
                 pos = x if m == 0 else y
                 pltpu.make_async_remote_copy(
-                    src_ref=stage.at[u, m, (c + dc) % CORES * side + (pos + step) % side],
-                    dst_ref=recv.at[m, it, pos, c, e],
+                    src_ref=stage.at[u, m, (c + dc) % CORES * side + (pos + step) % side, :, cols],
+                    dst_ref=recv.at[m, it, pos, c, e, :, cols],
                     send_sem=send_sem.at[u, m], recv_sem=recv_sem.at[m, it],
                     device_id=along(m, True, step, dc), device_id_type=MESH).start()
         for m in range(2):
             pos = x if m == 0 else y
-            pltpu.make_async_copy(stage.at[u, m, c * side + pos], recv.at[m, it, pos, c, e], recv_sem.at[m, it]).start()
+            pltpu.make_async_copy(stage.at[u, m, c * side + pos, :, cols],
+                                  recv.at[m, it, pos, c, e, :, cols], recv_sem.at[m, it]).start()
 
     def combine(m, it, meta_tile):
         ref = recv.at[m, it]
@@ -172,8 +184,7 @@
         ref = meta.at[m, it]
         pltpu.make_async_copy(ref, ref, meta_recv.at[m, it]).wait()
 
-    next_chunk()
-    next_chunk()
+    next_chunks(0)
 
     barrier = pltpu.get_barrier_semaphore()
     peers = 0
@@ -191,21 +202,19 @@
         kept = slots[...] >= 0
         own[m, :top_k, :tokens] = jnp.where(kept, experts[...] * cap + slots[...], -1).astype(jnp.float32)
         own[m, top_row:top_row + top_k, :tokens] = gates[...]
-    first_unit(0, 0)
-    pl.semaphore_wait(barrier, peers)
-    send_unit(0, 0, 0)
-    for m in range(2):
-        for it in range(side - 1):
-            step = side - turn * (2, 1, 3)[it]
-            pltpu.make_async_remote_copy(src_ref=own.at[m], dst_ref=meta.at[m, it], send_sem=meta_send.at[m, it],
-                                         recv_sem=meta_recv.at[m, it], device_id=along(m, False, step, 0),
-                                         device_id_type=MESH).start()
-
+    def meet():
+        pl.semaphore_wait(barrier, peers)
+        for m in range(2):
+            for it in range(side - 1):
+                step = side - turn * (2, 1, 3)[it]
+                pltpu.make_async_remote_copy(src_ref=own.at[m], dst_ref=meta.at[m, it], send_sem=meta_send.at[m, it],
+                                             recv_sem=meta_recv.at[m, it], device_id=along(m, False, step, 0),
+                                             device_id_type=MESH).start()
+
+    first_unit(0, 0, meet)
     for e in range(1, n_exp):
-        first_unit(e, e)
-        send_unit(e, 0, e)
-    for _ in range(side):
-        next_chunk()
+        first_unit(e, e, lambda: None)
+    next_chunks(side * n_exp * row_bytes)
 
     def send_far(m):
         for h, step in ((0, side + turn), (1, side - turn)):
@@ -228,28 +237,20 @@
             u = it * n_exp + e
             unit(u, e)
             send_unit(u, it, e)
-
-        @pl.when(it < side - 1)
+            if e == 0:
+                @pl.when(it == 1)
+                def _():
+                    for m in range(2):
+                        wait_meta(m, 0)
+                        combine(m, 0, meta[m, 0])
+                        send_far(m)
+
+        @pl.when(it == 2)
         def _():
             for m in range(2):
-                @pl.when(it == 1)
-                def _():
-                    wait_meta(m, 0)
-
-                @pl.when(it == 2)
-                def _():
-                    wait_meta(m, 1)
-                combine(m, it - 1, meta[m, it - 1])
-
-            @pl.when(it == 1)
-            def _():
-                for m in range(2):
-                    send_far(m)
-
-            @pl.when(it == 2)
-            def _():
-                for m in range(2):
-                    send_near(m, 1)
+                wait_meta(m, 1)
+                combine(m, 1, meta[m, 1])
+                send_near(m, 1)
         return carry
 
     lax.fori_loop(1, side, body, 0)
@@ -323,7 +324,7 @@
                 pltpu.VMEM((2, side, 2, tokens, dim // 2), jnp.float32),
                 pltpu.VMEM((2, 2, tokens, dim // 2), jnp.float32),
                 pltpu.VMEM((2, 2, 2, tokens, dim // 2), jnp.float32),
-                dma((units, 2)), dma((n_exp, 2 * (ffn // NT) + 2)), dma((n_exp, dim // DN)),
+                dma((units, 2)), dma((n_exp, len(TILES) + 1)), dma((n_exp, dim // DN)),
                 dma((units, 2)), dma((2, side)), dma((2, side - 1)), dma((2, side - 1)),
                 dma((2, 4)), dma((2, 2)), dma((2, 2)),
             ],

time: 83.6 us -> 83.1 us (level)
  no operation moved by 1% of the time
where the time goes in v4:
time: 83.1 us; the launch traced here: 83 us
  Pallas kernels  82.3 us (99%)
    pallas_call x1, Pallas kernels, local_step(): pl.pallas_call(functools.partial(moe_kernel, side), out_shape=(jax.ShapeD...  80.5 us
    pallas_call x1, Pallas kernels, local_step(): pl.pallas_call(copy_kernel, out_shape=(jax.ShapeDtypeStruct((tokens, dim)...  1.84 us

profile of v4, /device:TPU:97, one launch (start us, length us, event | category | flops | bytes accessed | tf_op | source)
XLA Modules:
  0.0 83.0 jit_solution(2436905841669857862)
XLA Ops:
  0.6 80.5 %shard_map.122 = (bf16[64,2048]{1,0:T(8,128)(2,1)}, bf16[64,2048]{1,0:T(8,128)(2,1)}) custom-call(bf16[4,4,2,2,16,2048]{5,4,3,2,1,0:T(8,128)(2,1)} %bitcast.8, bf16[4,4,2,2,16,2048]{5,4,3,2,1,0:T(8,128)(2,1)} %bitcast.9, s32[6,64]{1,0:T(8,128)} %bitcast.10, s32[6,64]{1,0:T(8,128)} %bitcast.11, s32[6,64]{1,0:T(8,128)} %bitcast.12, s32[6,64]{1,0:T(8,128)} %bitcast.13, ...), custom_call_target="tpu_custom_call" | custom-call | flops 35433480192 | bytes 43000000 | tf_op jit(solution)/shard_map/pallas_call | solution.py:311
  81.2 1.8 %shard_map.123 = (bf16[64,2048]{1,0:T(8,128)(2,1)}, bf16[64,2048]{1,0:T(8,128)(2,1)}) custom-call(bf16[64,2048]{1,0:T(8,128)(2,1)} %get-tuple-element.4.in_one, bf16[64,2048]{1,0:T(8,128)(2,1)} %get-tuple-element.5.in_two), custom_call_target="tpu_custom_call" | custom-call | tf_op jit(solution)/shard_map/pallas_call | solution.py:336
